TPU v7x, 32 devices: a whole 2x2x4 slice. The times are simulated.
32 devices in a mesh: atom: 8 (over z, x), energy: 4 (over y, core).
Axes of the slice: x: 2, y: 2, z: 4, core: 2. Of those that a mesh axis runs over, the one named last changes fastest.
Arguments:
- t_matrix: float32 [4, 64, 16, 16], P('energy', 'atom'), may hold values from -1.5 to 1.5
- structure: bfloat16 [4, 64, 1024, 1024], P('energy', 'atom'), may hold values from -0.125 to 0.125
- radial: bfloat16 [4, 64, 16, 1024], P('energy', 'atom'), may hold values from -3 to 3
- weights: float32 [4], P('energy'), may hold values from 0.1 to 1
- neighbours: int32 [64, 64], P('atom'), may hold values from 0 to 63, as said below
- live: int32 [64, 64], P('atom'), may hold values from 0 to 1, as said below
Outputs:
- density: float32 [64, 1024], P('atom', 'energy')
Inputs may be any that keep to these rules, and one draw needn't show every extreme that they name: `neighbours`: slot 0 of atom i holds i itself. Atom i lies at index i // 8 of the atom axis, and every neighbour of it lies at an index that differs from that one by at most 3 around the axis, which closes into a loop; both extremes occur in every draw. An atom may appear in several slots of one zone. `live`: each row is 1 on its first slots and 0 after; slot 0 is always 1, at least 16 slots are 1, and some atom has all 64 slots 1.
All inputs are finite; a program needn't handle non-finite values.
Results may differ from a plain program's by a relative error of at most 0.0043.
Values sent between devices are 32-bit elements; how exact they have to be, the bound alone decides.
No kernel may reach another device: no remote copies, remote signals or barrier semaphores. Data moves between devices by JAX's collectives and lax.ppermute only.
A program may use at most 128 MiB of HBM per device.

v0:
```python
import functools

import jax
import jax.numpy as jnp
from jax import lax
from jax.experimental import pallas as pl
from jax.experimental.pallas import tpu as pltpu
from jax.sharding import PartitionSpec as P

ITERS = 4
SPAN = 3
TILE = 256
N_ACC = 4


def shifted(value, axis, by):
    devices = lax.axis_size(axis)
    return lax.ppermute(value, axis, [(i, (i + by) % devices) for i in range(devices)])


def dot_nt(a, b):
    return lax.dot_general(a, b, (((1,), (1,)), ((), ())), preferred_element_type=jnp.float32)


def zone_kernel(dims, idx_ref, first_ref, g_hbm, *refs):
    a_dev, zone, lm, places = dims
    t_refs = refs[:places]
    out_ref = refs[places]
    g, tab, bd, mask, img, colb, fin = refs[places + 1 : places + 8]
    accs = refs[places + 8 : places + 8 + N_ACC]
    sems = refs[places + 8 + N_ACC]
    width = zone * lm
    n_q = width // TILE
    per = TILE // lm
    rows = a_dev * lm

    def copy(a):
        return pltpu.make_async_copy(g_hbm.at[a], g.at[a], sems.at[a])

    for a in range(a_dev):
        copy(a).start()
    for acc in accs:
        acc[...] = jnp.zeros(acc.shape, jnp.float32)
    row_i = lax.broadcasted_iota(jnp.int32, (TILE, TILE), 0)
    col_i = lax.broadcasted_iota(jnp.int32, (TILE, TILE), 1)
    mask[...] = jnp.where(row_i // lm == col_i // lm, 1.0, 0.0).astype(jnp.bfloat16)
    rep_r = lax.broadcasted_iota(jnp.int32, (lm, TILE), 0)
    rep_c = lax.broadcasted_iota(jnp.int32, (lm, TILE), 1)
    rep = jnp.where(rep_r == rep_c % lm, 1.0, 0.0).astype(jnp.bfloat16)
    for p in range(places):
        piece = t_refs[p][...].reshape(rows, lm).astype(jnp.bfloat16)
        wide = jnp.dot(piece, rep, preferred_element_type=jnp.float32)
        tab[p * rows : (p + 1) * rows, :] = wide.astype(jnp.bfloat16)
    tab[places * rows : places * rows + lm, :] = jnp.zeros((lm, TILE), jnp.bfloat16)

    def build(a, carry):
        for s in range(zone):
            at = pl.multiple_of(idx_ref[a, s] * lm, lm)
            m = s % per
            bd[a, s * lm : (s + 1) * lm, :] = tab[pl.ds(at, lm), :] * mask[m * lm : (m + 1) * lm, :]
        return carry

    lax.fori_loop(0, a_dev, build, 0)

    for a in range(a_dev):
        copy(a).wait()
        img[a] = dot_nt(first_ref[a].astype(jnp.bfloat16), g[a, :, :TILE]).astype(jnp.bfloat16)

    def sweep(step, carry):
        for a in range(a_dev):
            for q in range(n_q):
                cut = slice(q * TILE, (q + 1) * TILE)
                c = dot_nt(img[a, :, cut], bd[a, cut, :])
                if q == 0:
                    c = c + first_ref[a]
                colb[a, :, cut] = c.astype(jnp.bfloat16)
        for a in range(a_dev):
            img[a] = dot_nt(colb[a], g[a]).astype(jnp.bfloat16)
        return carry

    lax.fori_loop(0, ITERS - 1, sweep, 0)

    for a in range(a_dev):
        for q in range(n_q):
            cut = slice(q * TILE, (q + 1) * TILE)
            f = dot_nt(bd[a, cut, :], img[a, :, cut])
            fin[a, cut, :] = f
        fin[a, :lm, :] = fin[a, :lm, :] + t_refs[SPAN][a]

    def scatter(a, carry):
        for s in range(zone):
            at = pl.multiple_of(idx_ref[a, s] * lm, lm)
            acc = accs[s % N_ACC]
            acc[pl.ds(at, lm), :] = acc[pl.ds(at, lm), :] + fin[a, s * lm : (s + 1) * lm, :]
        return carry

    lax.fori_loop(0, a_dev, scatter, 0)

    for p in range(places):
        total = accs[0][p * rows : (p + 1) * rows, :]
        for acc in accs[1:]:
            total = total + acc[p * rows : (p + 1) * rows, :]
        out_ref[p] = jnp.concatenate([total[a * lm : (a + 1) * lm] for a in range(a_dev)], axis=1)


def density_kernel(dims, me_ref, w_ref, *refs):
    a_dev, lm, places, parts = dims
    pieces = refs[:places]
    radial_ref = refs[places]
    outs = refs[places + 1 : places + 1 + parts]
    buf = refs[places + 1 + parts]
    total = pieces[0][...]
    for piece in pieces[1:]:
        total = total + piece[...]
    rows = a_dev * lm
    tall = jnp.concatenate([total] * a_dev, axis=0)
    row_i = lax.broadcasted_iota(jnp.int32, (rows, rows), 0)
    col_i = lax.broadcasted_iota(jnp.int32, (rows, rows), 1)
    block = jnp.where(row_i // lm == col_i // lm, tall, 0.0).astype(jnp.bfloat16)
    radial = radial_ref[...].reshape(rows, -1)
    turned = jnp.dot(block, radial, preferred_element_type=jnp.float32)
    prod = turned * radial.astype(jnp.float32)
    buf[...] = w_ref[0] * jnp.sum(prod.reshape(a_dev, lm, -1), axis=1)
    cut = buf.shape[1] // parts
    for d in range(parts):
        at = pl.multiple_of(((me_ref[0] + d) % parts) * cut, cut)
        outs[d][...] = buf[:, pl.ds(at, cut)]


def shards(t_matrix, structure, radial, weights, neighbours, live):
    a_dev, lm = t_matrix.shape[1], t_matrix.shape[2]
    zone = neighbours.shape[1]
    n_r = radial.shape[3]
    n_atom = lax.axis_size("atom")
    n_energy = lax.axis_size("energy")
    me = lax.axis_index("atom")
    places = 2 * SPAN + 1
    width = zone * lm
    rows = a_dev * lm
    t_own = t_matrix[0]
    pieces = [t_own] * places
    for place in range(places):
        if place != SPAN:
            pieces[place] = shifted(t_own, "atom", SPAN - place)
    place_of = (neighbours // a_dev - me + SPAN + n_atom) % n_atom
    target = place_of * a_dev + neighbours % a_dev
    index = jnp.where(live != 0, target, a_dev * places)
    first = jnp.pad(jnp.swapaxes(t_own, 1, 2), ((0, 0), (0, 0), (0, TILE - lm)))

    smem = pl.BlockSpec(memory_space=pltpu.SMEM)
    vmem = pl.BlockSpec(memory_space=pltpu.VMEM)
    acc_shape = pltpu.VMEM(((places * a_dev + 1) * lm, lm), jnp.float32)
    sent = pl.pallas_call(
        functools.partial(zone_kernel, (a_dev, zone, lm, places)),
        name="zone",
        out_shape=jax.ShapeDtypeStruct((places, lm, rows), jnp.float32),
        in_specs=[smem, vmem, pl.BlockSpec(memory_space=pl.ANY)] + [vmem] * places,
        out_specs=vmem,
        scratch_shapes=[
            pltpu.VMEM((a_dev, width, width), jnp.bfloat16),
            pltpu.VMEM(((places * a_dev + 1) * lm, TILE), jnp.bfloat16),
            pltpu.VMEM((a_dev, width, TILE), jnp.bfloat16),
            pltpu.VMEM((TILE, TILE), jnp.bfloat16),
            pltpu.VMEM((a_dev, lm, width), jnp.bfloat16),
            pltpu.VMEM((a_dev, lm, width), jnp.bfloat16),
            pltpu.VMEM((a_dev, width, lm), jnp.float32),
        ]
        + [acc_shape] * N_ACC
        + [pltpu.SemaphoreType.DMA((a_dev,))],
        compiler_params=pltpu.CompilerParams(vmem_limit_bytes=48 * 1024 * 1024),
    )(index, first, structure[0], *pieces)

    got = [sent[SPAN]]
    for place in range(places):
        if place != SPAN:
            got.append(shifted(sent[place], "atom", place - SPAN))
    cut = n_r // n_energy
    mine = lax.axis_index("energy").astype(jnp.int32).reshape(1)
    chunks = pl.pallas_call(
        functools.partial(density_kernel, (a_dev, lm, places, n_energy)),
        name="density",
        out_shape=[jax.ShapeDtypeStruct((a_dev, cut), jnp.float32)] * n_energy,
        in_specs=[smem, smem] + [vmem] * (places + 1),
        out_specs=[vmem] * n_energy,
        scratch_shapes=[pltpu.VMEM((a_dev, n_r), jnp.float32)],
    )(mine, weights, *got, radial[0])
    total = chunks[0]
    for d in range(1, n_energy):
        total = total + shifted(chunks[d], "energy", d)
    return total


def solution(mesh):
    in_specs = (
        P("energy", "atom", None, None),
        P("energy", "atom", None, None),
        P("energy", "atom", None, None),
        P("energy"),
        P("atom", None),
        P("atom", None),
    )
    out_specs = P("atom", "energy")
    return jax.shard_map(shards, mesh=mesh, in_specs=in_specs, out_specs=out_specs, check_vma=False)
```

profile of v0, /device:TPU:7, one launch (start us, length us, event | category | flops | bytes accessed | tf_op | source)
XLA Modules:
  0.0 65.4 jit_solution(5500779294214791664)
XLA Ops:
  0.0 3.3 %collective-permute-start.5 = (f32[8,16,16]{2,1,0:T(8,128)}, f32[8,16,16]{2,1,0:T(8,128)S(1)}, u32[]{:S(2)}, u32[]{:S(2)}) collective-permute-start(f32[8,16,16]{2,1,0:T(8,128)} %bitcast.20), channel_id=1, source_target_pairs={{0,20},{4,24},{8,28},{12,0},{16,4},{20,8},{24,12},{28,16},{1,21},{... | collective-permute-start | bytes 24584 | tf_op jit(solution)/shard_map/ppermute | solution.py:18
  3.3 0.2 collective-permute-start.4
  3.5 1.1 %collective-permute-start.3 = (f32[8,16,16]{2,1,0:T(8,128)}, f32[8,16,16]{2,1,0:T(8,128)S(1)}, u32[]{:S(2)}, u32[]{:S(2)}) collective-permute-start(f32[8,16,16]{2,1,0:T(8,128)} %bitcast.22), channel_id=1, source_target_pairs={{0,28},{4,0},{8,4},{12,8},{16,12},{20,16},{24,20},{28,24},{1,29},{... | collective-permute-start | bytes 24584 | tf_op jit(solution)/shard_map/ppermute | solution.py:18
  4.6 1.3 %collective-permute-start.2 = (f32[8,16,16]{2,1,0:T(8,128)}, f32[8,16,16]{2,1,0:T(8,128)S(1)}, u32[]{:S(2)}, u32[]{:S(2)}) collective-permute-start(f32[8,16,16]{2,1,0:T(8,128)} %bitcast.23), channel_id=1, source_target_pairs={{0,4},{4,8},{8,12},{12,16},{16,20},{20,24},{24,28},{28,0},{1,5},{5... | collective-permute-start | bytes 24584 | tf_op jit(solution)/shard_map/ppermute | solution.py:18
  5.8 1.3 %collective-permute-start.1 = (f32[8,16,16]{2,1,0:T(8,128)}, f32[8,16,16]{2,1,0:T(8,128)S(1)}, u32[]{:S(2)}, u32[]{:S(2)}) collective-permute-start(f32[8,16,16]{2,1,0:T(8,128)} %bitcast.24), channel_id=1, source_target_pairs={{0,8},{4,12},{8,16},{12,20},{16,24},{20,28},{24,0},{28,4},{1,9},{5... | collective-permute-start | bytes 24584 | tf_op jit(solution)/shard_map/ppermute | solution.py:18
  7.1 0.0 collective-permute-done.5.refs_6_
  7.1 0.0 collective-permute-start
  7.2 0.7 %fusion.5.idx_ref = s32[8,64]{1,0:T(8,128)S(1)} fusion(s32[8,64]{1,0:T(8,128)} %param.10, s32[8,64]{1,0:T(8,128)} %param.11, s32[]{:T(128)S(6)} %axis_index.25), kind=kLoop, calls=%fused_computation.21 | loop fusion | flops 18432 | bytes 6148 | tf_op jit(solution)/shard_map/jit(_where)/select_n | solution.py:147
  7.9 0.9 %copy.8 = f32[8,16,16]{2,1,0:T(8,128)S(1)} copy(f32[8,16,16]{1,2,0:T(8,128)} %bitcast.26) | data formatting | bytes 16384
  8.8 0.0 collective-permute-done.4.refs_5_
  8.8 0.0 collective-permute-done.3.refs_4_
  8.8 0.0 collective-permute-done.2.refs_2_
  8.9 2.2 %collective-permute-done.1.refs_1_ = f32[8,16,16]{2,1,0:T(8,128)S(1)} collective-permute-done((f32[8,16,16]{2,1,0:T(8,128)}, f32[8,16,16]{2,1,0:T(8,128)S(1)}, u32[]{:S(2)}, u32[]{:S(2)}) %collective-permute-start.1) | collective-permute-done | bytes 8224 | tf_op jit(solution)/shard_map/ppermute | solution.py:18
  11.1 2.7 %collective-permute-done.refs_0_ = f32[8,16,16]{2,1,0:T(8,128)S(1)} collective-permute-done((f32[8,16,16]{2,1,0:T(8,128)}, f32[8,16,16]{2,1,0:T(8,128)S(1)}, u32[]{:S(2)}, u32[]{:S(2)}) %collective-permute-start) | collective-permute-done | bytes 8224 | tf_op jit(solution)/shard_map/ppermute | solution.py:18
  13.8 0.0 copy-start
  13.8 0.8 %copy-done = f32[1,8,16,16]{3,2,1,0:T(8,128)S(1)} copy-done((f32[1,8,16,16]{3,2,1,0:T(8,128)S(1)}, f32[1,8,16,16]{3,2,1,0:T(8,128)}, u32[]{:S(2)}) %copy-start) | copy-done | bytes 8216
  14.7 25.8 %zone.1 = f32[7,16,128]{2,1,0:T(8,128)S(1)} custom-call(s32[8,64]{1,0:T(8,128)S(1)} %fusion.5.idx_ref, f32[8,16,256]{2,1,0:T(8,128)S(1)} %pad.4.clone.first_ref, bf16[8,1024,1024]{2,1,0:T(8,128)(2,1)} %bitcast.28, f32[8,16,16]{2,1,0:T(8,128)S(1)} %collective-permute-done.refs_0_, f32[8,16,16]{2,1,0:T(8,128)S(1)} %collective-permute-done.1.refs_1_, ...), custom_call_target="tpu_custom_call" | custom-call | tf_op jit(solution)/shard_map/zone/pallas_call | solution.py:153
  40.5 0.6 slice_bitcast_fusion
  41.1 2.2 %collective-permute-start.11 = (f32[16,128]{1,0:T(8,128)S(1)}, f32[16,128]{1,0:T(8,128)S(1)}, u32[]{:S(2)}, u32[]{:S(2)}) collective-permute-start(f32[16,128]{1,0:T(8,128)S(1)} %get-tuple-element.13), channel_id=1, source_target_pairs={{0,12},{4,16},{8,20},{12,24},{16,28},{20,0},{24,4},{28,8},{1,13},{... | collective-permute-start | bytes 24584 | tf_op jit(solution)/shard_map/ppermute | solution.py:18
  43.4 0.5 collective-permute-start.10
  43.9 2.3 %collective-permute-start.9 = (f32[16,128]{1,0:T(8,128)S(1)}, f32[16,128]{1,0:T(8,128)S(1)}, u32[]{:S(2)}, u32[]{:S(2)}) collective-permute-start(f32[16,128]{1,0:T(8,128)S(1)} %get-tuple-element.15), channel_id=1, source_target_pairs={{0,4},{4,8},{8,12},{12,16},{16,20},{20,24},{24,28},{28,0},{1,5},{5... | collective-permute-start | bytes 24584 | tf_op jit(solution)/shard_map/ppermute | solution.py:18
  46.2 0.0 collective-permute-start.8
  46.2 1.9 %collective-permute-start.7 = (f32[16,128]{1,0:T(8,128)S(1)}, f32[16,128]{1,0:T(8,128)S(1)}, u32[]{:S(2)}, u32[]{:S(2)}) collective-permute-start(f32[16,128]{1,0:T(8,128)S(1)} %get-tuple-element.17), channel_id=1, source_target_pairs={{0,24},{4,28},{8,0},{12,4},{16,8},{20,12},{24,16},{28,20},{1,25},{... | collective-permute-start | bytes 24584 | tf_op jit(solution)/shard_map/ppermute | solution.py:18
  48.1 0.0 collective-permute-done.11.refs_6_
  48.1 1.3 %collective-permute-start.6 = (f32[16,128]{1,0:T(8,128)S(1)}, f32[16,128]{1,0:T(8,128)S(1)}, u32[]{:S(2)}, u32[]{:S(2)}) collective-permute-start(f32[16,128]{1,0:T(8,128)S(1)} %get-tuple-element.18), channel_id=1, source_target_pairs={{0,20},{4,24},{8,28},{12,0},{16,4},{20,8},{24,12},{28,16},{1,21},{... | collective-permute-start | bytes 24584 | tf_op jit(solution)/shard_map/ppermute | solution.py:18
  50.1 0.0 collective-permute-done.10.refs_5_
  50.1 0.0 copy-start.2
  50.1 0.0 collective-permute-done.9.refs_4_
  50.1 0.0 copy-start.3
  50.1 0.0 collective-permute-done.8.refs_3_
  50.1 0.0 copy-start.4
  50.1 0.0 collective-permute-done.7.refs_2_
  50.2 0.0 copy-start.5
  50.2 2.2 %collective-permute-done.6.refs_1_ = f32[16,128]{1,0:T(8,128)S(1)} collective-permute-done((f32[16,128]{1,0:T(8,128)S(1)}, f32[16,128]{1,0:T(8,128)S(1)}, u32[]{:S(2)}, u32[]{:S(2)}) %collective-permute-start.6) | collective-permute-done | bytes 8224 | tf_op jit(solution)/shard_map/ppermute | solution.py:18
  52.4 0.0 copy-done.1
  52.4 0.0 copy-done.2
  52.4 0.0 copy-done.3
  52.4 0.0 copy-done.4
  52.4 0.0 copy-done.5
  52.4 0.6 copy-done.6
  53.0 1.9 %density.1 = (f32[8,256]{1,0:T(8,128)}, f32[8,256]{1,0:T(8,128)}, f32[8,256]{1,0:T(8,128)}, f32[8,256]{1,0:T(8,128)}) custom-call(s32[1]{0:T(128)} %bitcast.me_ref, f32[1]{0:T(128)S(6)} %copy.9.w_ref, f32[16,128]{1,0:T(8,128)} %get-tuple-element.19.refs_0_, f32[16,128]{1,0:T(8,128)} %copy-done.6, f32[16,128]{1,0:T(8,128)} %copy-done.5, f32[16,128]{1,0:T(8,128)} %copy-done.4, ...), custom_call_target="tpu_custom_call" | custom-call | tf_op jit(solution)/shard_map/density/pallas_call | solution.py:179
  54.9 4.6 %collective-permute-start.12 = (f32[8,256]{1,0:T(8,128)}, f32[8,256]{1,0:T(8,128)S(1)}, u32[]{:S(2)}, u32[]{:S(2)}) collective-permute-start(f32[8,256]{1,0:T(8,128)} %get-tuple-element.10), channel_id=1, source_target_pairs={{0,1},{1,2},{2,3},{3,0},{4,5},{5,6},{6,7},{7,4},{8,9},{9,10},{10,1... | collective-permute-start | bytes 24584 | tf_op jit(solution)/shard_map/ppermute | solution.py:18
  59.6 1.2 %collective-permute-start.13 = (f32[8,256]{1,0:T(8,128)}, f32[8,256]{1,0:T(8,128)S(1)}, u32[]{:S(2)}, u32[]{:S(2)}) collective-permute-start(f32[8,256]{1,0:T(8,128)} %get-tuple-element.11), channel_id=1, source_target_pairs={{0,2},{1,3},{2,0},{3,1},{4,6},{5,7},{6,4},{7,5},{8,10},{9,11},{10,... | collective-permute-start | bytes 24584 | tf_op jit(solution)/shard_map/ppermute | solution.py:18
  60.8 0.0 collective-permute-start.14
  60.8 0.0 collective-permute-done.12
  60.8 1.5 %collective-permute-done.13 = f32[8,256]{1,0:T(8,128)S(1)} collective-permute-done((f32[8,256]{1,0:T(8,128)}, f32[8,256]{1,0:T(8,128)S(1)}, u32[]{:S(2)}, u32[]{:S(2)}) %collective-permute-start.13) | collective-permute-done | bytes 8224 | tf_op jit(solution)/shard_map/ppermute | solution.py:18
  62.3 1.7 %collective-permute-done.14 = f32[8,256]{1,0:T(8,128)S(1)} collective-permute-done((f32[8,256]{1,0:T(8,128)}, f32[8,256]{1,0:T(8,128)S(1)}, u32[]{:S(2)}, u32[]{:S(2)}) %collective-permute-start.14) | collective-permute-done | bytes 8224 | tf_op jit(solution)/shard_map/ppermute | solution.py:18
  64.1 1.3 %add_add_fusion = f32[8,256]{1,0:T(8,128)} fusion(f32[8,256]{1,0:T(8,128)S(1)} %collective-permute-done.14, f32[8,256]{1,0:T(8,128)S(1)} %collective-permute-done.13, f32[8,256]{1,0:T(8,128)} %get-tuple-element.9, f32[8,256]{1,0:T(8,128)S(1)} %collective-permute-done.12), kind=kLoop, calls=%fused_computation.7 | loop fusion | flops 6144 | bytes 40960 | tf_op jit(solution)/shard_map/add | solution.py:189
  (3 shorter events, 0.0 us)
Async XLA Ops:
  0.0 7.1 %collective-permute-start.5 = (f32[8,16,16]{2,1,0:T(8,128)}, f32[8,16,16]{2,1,0:T(8,128)S(1)}, u32[]{:S(2)}, u32[]{:S(2)}) collective-permute-start(f32[8,16,16]{2,1,0:T(8,128)} %bitcast.20), channel_id=1, source_target_pairs={{0,20},{4,24},{8,28},{12,0},{16,4},{20,8},{24,12},{28,16},{1,21},{... | collective-permute-start | bytes 24584 | tf_op jit(solution)/shard_map/ppermute | solution.py:18
  3.3 5.5 %collective-permute-start.4 = (f32[8,16,16]{2,1,0:T(8,128)}, f32[8,16,16]{2,1,0:T(8,128)S(1)}, u32[]{:S(2)}, u32[]{:S(2)}) collective-permute-start(f32[8,16,16]{2,1,0:T(8,128)} %bitcast.21), channel_id=1, source_target_pairs={{0,24},{4,28},{8,0},{12,4},{16,8},{20,12},{24,16},{28,20},{1,25},{... | collective-permute-start | bytes 24584 | tf_op jit(solution)/shard_map/ppermute | solution.py:18
  3.5 5.4 %collective-permute-start.3 = (f32[8,16,16]{2,1,0:T(8,128)}, f32[8,16,16]{2,1,0:T(8,128)S(1)}, u32[]{:S(2)}, u32[]{:S(2)}) collective-permute-start(f32[8,16,16]{2,1,0:T(8,128)} %bitcast.22), channel_id=1, source_target_pairs={{0,28},{4,0},{8,4},{12,8},{16,12},{20,16},{24,20},{28,24},{1,29},{... | collective-permute-start | bytes 24584 | tf_op jit(solution)/shard_map/ppermute | solution.py:18
  4.6 4.3 %collective-permute-start.2 = (f32[8,16,16]{2,1,0:T(8,128)}, f32[8,16,16]{2,1,0:T(8,128)S(1)}, u32[]{:S(2)}, u32[]{:S(2)}) collective-permute-start(f32[8,16,16]{2,1,0:T(8,128)} %bitcast.23), channel_id=1, source_target_pairs={{0,4},{4,8},{8,12},{12,16},{16,20},{20,24},{24,28},{28,0},{1,5},{5... | collective-permute-start | bytes 24584 | tf_op jit(solution)/shard_map/ppermute | solution.py:18
  5.8 5.2 %collective-permute-start.1 = (f32[8,16,16]{2,1,0:T(8,128)}, f32[8,16,16]{2,1,0:T(8,128)S(1)}, u32[]{:S(2)}, u32[]{:S(2)}) collective-permute-start(f32[8,16,16]{2,1,0:T(8,128)} %bitcast.24), channel_id=1, source_target_pairs={{0,8},{4,12},{8,16},{12,20},{16,24},{20,28},{24,0},{28,4},{1,9},{5... | collective-permute-start | bytes 24584 | tf_op jit(solution)/shard_map/ppermute | solution.py:18
  7.1 6.7 %collective-permute-start = (f32[8,16,16]{2,1,0:T(8,128)}, f32[8,16,16]{2,1,0:T(8,128)S(1)}, u32[]{:S(2)}, u32[]{:S(2)}) collective-permute-start(f32[8,16,16]{2,1,0:T(8,128)} %bitcast.25), channel_id=1, source_target_pairs={{0,12},{4,16},{8,20},{12,24},{16,28},{20,0},{24,4},{28,8},{1,13},{... | collective-permute-start | bytes 24584 | tf_op jit(solution)/shard_map/ppermute | solution.py:18
  13.8 0.8 %copy-start = (f32[1,8,16,16]{3,2,1,0:T(8,128)S(1)}, f32[1,8,16,16]{3,2,1,0:T(8,128)}, u32[]{:S(2)}) copy-start(f32[1,8,16,16]{3,2,1,0:T(8,128)} %param.6) | copy-start | bytes 24580
  41.1 7.0 %collective-permute-start.11 = (f32[16,128]{1,0:T(8,128)S(1)}, f32[16,128]{1,0:T(8,128)S(1)}, u32[]{:S(2)}, u32[]{:S(2)}) collective-permute-start(f32[16,128]{1,0:T(8,128)S(1)} %get-tuple-element.13), channel_id=1, source_target_pairs={{0,12},{4,16},{8,20},{12,24},{16,28},{20,0},{24,4},{28,8},{1,13},{... | collective-permute-start | bytes 24584 | tf_op jit(solution)/shard_map/ppermute | solution.py:18
  43.4 6.7 %collective-permute-start.10 = (f32[16,128]{1,0:T(8,128)S(1)}, f32[16,128]{1,0:T(8,128)S(1)}, u32[]{:S(2)}, u32[]{:S(2)}) collective-permute-start(f32[16,128]{1,0:T(8,128)S(1)} %get-tuple-element.14), channel_id=1, source_target_pairs={{0,8},{4,12},{8,16},{12,20},{16,24},{20,28},{24,0},{28,4},{1,9},{5... | collective-permute-start | bytes 24584 | tf_op jit(solution)/shard_map/ppermute | solution.py:18
  43.9 6.2 %collective-permute-start.9 = (f32[16,128]{1,0:T(8,128)S(1)}, f32[16,128]{1,0:T(8,128)S(1)}, u32[]{:S(2)}, u32[]{:S(2)}) collective-permute-start(f32[16,128]{1,0:T(8,128)S(1)} %get-tuple-element.15), channel_id=1, source_target_pairs={{0,4},{4,8},{8,12},{12,16},{16,20},{20,24},{24,28},{28,0},{1,5},{5... | collective-permute-start | bytes 24584 | tf_op jit(solution)/shard_map/ppermute | solution.py:18
  46.2 4.0 %collective-permute-start.8 = (f32[16,128]{1,0:T(8,128)S(1)}, f32[16,128]{1,0:T(8,128)S(1)}, u32[]{:S(2)}, u32[]{:S(2)}) collective-permute-start(f32[16,128]{1,0:T(8,128)S(1)} %get-tuple-element.16), channel_id=1, source_target_pairs={{0,28},{4,0},{8,4},{12,8},{16,12},{20,16},{24,20},{28,24},{1,29},{... | collective-permute-start | bytes 24584 | tf_op jit(solution)/shard_map/ppermute | solution.py:18
  46.2 4.0 %collective-permute-start.7 = (f32[16,128]{1,0:T(8,128)S(1)}, f32[16,128]{1,0:T(8,128)S(1)}, u32[]{:S(2)}, u32[]{:S(2)}) collective-permute-start(f32[16,128]{1,0:T(8,128)S(1)} %get-tuple-element.17), channel_id=1, source_target_pairs={{0,24},{4,28},{8,0},{12,4},{16,8},{20,12},{24,16},{28,20},{1,25},{... | collective-permute-start | bytes 24584 | tf_op jit(solution)/shard_map/ppermute | solution.py:18
  48.1 4.3 %copy-start.1 = (f32[16,128]{1,0:T(8,128)}, f32[16,128]{1,0:T(8,128)S(1)}, u32[]{:S(2)}) copy-start(f32[16,128]{1,0:T(8,128)S(1)} %collective-permute-done.11.refs_6_) | copy-start | bytes 24580
  48.1 4.3 %collective-permute-start.6 = (f32[16,128]{1,0:T(8,128)S(1)}, f32[16,128]{1,0:T(8,128)S(1)}, u32[]{:S(2)}, u32[]{:S(2)}) collective-permute-start(f32[16,128]{1,0:T(8,128)S(1)} %get-tuple-element.18), channel_id=1, source_target_pairs={{0,20},{4,24},{8,28},{12,0},{16,4},{20,8},{24,12},{28,16},{1,21},{... | collective-permute-start | bytes 24584 | tf_op jit(solution)/shard_map/ppermute | solution.py:18
  50.1 2.3 %copy-start.2 = (f32[16,128]{1,0:T(8,128)}, f32[16,128]{1,0:T(8,128)S(1)}, u32[]{:S(2)}) copy-start(f32[16,128]{1,0:T(8,128)S(1)} %collective-permute-done.10.refs_5_) | copy-start | bytes 24580
  50.1 2.3 %copy-start.3 = (f32[16,128]{1,0:T(8,128)}, f32[16,128]{1,0:T(8,128)S(1)}, u32[]{:S(2)}) copy-start(f32[16,128]{1,0:T(8,128)S(1)} %collective-permute-done.9.refs_4_) | copy-start | bytes 24580
  50.1 2.3 %copy-start.4 = (f32[16,128]{1,0:T(8,128)}, f32[16,128]{1,0:T(8,128)S(1)}, u32[]{:S(2)}) copy-start(f32[16,128]{1,0:T(8,128)S(1)} %collective-permute-done.8.refs_3_) | copy-start | bytes 24580
  50.2 2.3 %copy-start.5 = (f32[16,128]{1,0:T(8,128)}, f32[16,128]{1,0:T(8,128)S(1)}, u32[]{:S(2)}) copy-start(f32[16,128]{1,0:T(8,128)S(1)} %collective-permute-done.7.refs_2_) | copy-start | bytes 24580
  52.4 0.6 copy-start.6
  54.9 5.9 %collective-permute-start.12 = (f32[8,256]{1,0:T(8,128)}, f32[8,256]{1,0:T(8,128)S(1)}, u32[]{:S(2)}, u32[]{:S(2)}) collective-permute-start(f32[8,256]{1,0:T(8,128)} %get-tuple-element.10), channel_id=1, source_target_pairs={{0,1},{1,2},{2,3},{3,0},{4,5},{5,6},{6,7},{7,4},{8,9},{9,10},{10,1... | collective-permute-start | bytes 24584 | tf_op jit(solution)/shard_map/ppermute | solution.py:18
  59.6 2.8 %collective-permute-start.13 = (f32[8,256]{1,0:T(8,128)}, f32[8,256]{1,0:T(8,128)S(1)}, u32[]{:S(2)}, u32[]{:S(2)}) collective-permute-start(f32[8,256]{1,0:T(8,128)} %get-tuple-element.11), channel_id=1, source_target_pairs={{0,2},{1,3},{2,0},{3,1},{4,6},{5,7},{6,4},{7,5},{8,10},{9,11},{10,... | collective-permute-start | bytes 24584 | tf_op jit(solution)/shard_map/ppermute | solution.py:18
  60.8 3.3 %collective-permute-start.14 = (f32[8,256]{1,0:T(8,128)}, f32[8,256]{1,0:T(8,128)S(1)}, u32[]{:S(2)}, u32[]{:S(2)}) collective-permute-start(f32[8,256]{1,0:T(8,128)} %get-tuple-element.12), channel_id=1, source_target_pairs={{0,3},{1,0},{2,1},{3,2},{4,7},{5,4},{6,5},{7,6},{8,11},{9,8},{10,9... | collective-permute-start | bytes 24584 | tf_op jit(solution)/shard_map/ppermute | solution.py:18
where the time goes:
time: 65.7 us; the launch traced here: 65.4 us
  Pallas kernels  27.8 us (42%)
  starting transfers between devices  21.3 us (32%)
  waiting for transfers between devices  10.5 us (16%)
  local copies, waits for them, and re-layouts  2.96 us (5%)
  other arithmetic  2.02 us (3%)
  between operations  0.79 us (1%)
    pallas_call x1, Pallas kernels, shards(): pl.pallas_call(functools.partial(zone_kernel, (a_dev, zone, lm, places)),...  25.8 us
    ppermute x15, starting transfers between devices, shifted(): lax.ppermute(value, axis, [(i, (i + by) % devices) for i in range(devices)])  21.3 us
    ppermute x15, waiting for transfers between devices, shifted(): lax.ppermute(value, axis, [(i, (i + by) % devices) for i in range(devices)])  10.5 us
    unnamed x15, local copies, waits for them, and re-layouts  2.34 us
    pallas_call x1, Pallas kernels, shards(): pl.pallas_call(functools.partial(density_kernel, (a_dev, lm, places, n_en...  1.94 us
  transfers between devices with their start and end apart: 15, of which 5 were waited for; matrix products, arithmetic and copies ran while one was open for 3% of the time, Pallas kernels for 0%

commit v1 on v0

--- a/solution.py
+++ b/solution.py
@@ -183,6 +183,7 @@
         in_specs=[smem, smem] + [vmem] * (places + 1),
         out_specs=[vmem] * n_energy,
         scratch_shapes=[pltpu.VMEM((a_dev, n_r), jnp.float32)],
+        compiler_params=pltpu.CompilerParams(vmem_limit_bytes=8 * 1024 * 1024),
     )(mine, weights, *got, radial[0])
     total = chunks[0]
     for d in range(1, n_energy):

time: 65.7 us -> 62 us (0.944)
  Pallas kernels: 27.8 us -> 26.1 us
  local copies, waits for them, and re-layouts: 2.96 us -> 1.78 us
  other arithmetic: 2.02 us -> 1.33 us
    pallas_call x1, Pallas kernels: 1.94 us -> 0.26 us  [shards(): pl.pallas_call(functools.partial(density_kernel, (a_dev, lm, places, n_en...]
    add x1, other arithmetic: 1.3 us -> 0.6 us  [shards(): total = total + shifted(chunks[d], 'energy', d)]
    unnamed x15 -> x5, local copies, waits for them, and re-layouts: 2.34 us -> 1.76 us
where the time goes in v1:
time: 62 us; the launch traced here: 61.7 us
  Pallas kernels  26.1 us (42%)
  starting transfers between devices  21.4 us (35%)
  waiting for transfers between devices  10.3 us (17%)
  local copies, waits for them, and re-layouts  1.78 us (3%)
  other arithmetic  1.33 us (2%)
  between operations  0.75 us (1%)
    pallas_call x1, Pallas kernels, shards(): pl.pallas_call(functools.partial(zone_kernel, (a_dev, zone, lm, places)),...  25.8 us
    ppermute x15, starting transfers between devices, shifted(): lax.ppermute(value, axis, [(i, (i + by) % devices) for i in range(devices)])  21.4 us
    ppermute x15, waiting for transfers between devices, shifted(): lax.ppermute(value, axis, [(i, (i + by) % devices) for i in range(devices)])  10.3 us
    unnamed x5, local copies, waits for them, and re-layouts  1.76 us
  transfers between devices with their start and end apart: 15, of which 5 were waited for; matrix products, arithmetic and copies ran while one was open for 3% of the time, Pallas kernels for 0%

profile of v1, /device:TPU:7, one launch (start us, length us, event | category | flops | bytes accessed | tf_op | source)
XLA Modules:
  0.0 61.7 jit_solution(8405878060155118794)
XLA Ops:
  0.0 0.0 copy-start
  0.0 3.3 %collective-permute-start.5 = (f32[8,16,16]{2,1,0:T(8,128)}, f32[8,16,16]{2,1,0:T(8,128)S(1)}, u32[]{:S(2)}, u32[]{:S(2)}) collective-permute-start(f32[8,16,16]{2,1,0:T(8,128)} %bitcast.21), channel_id=1, source_target_pairs={{0,20},{4,24},{8,28},{12,0},{16,4},{20,8},{24,12},{28,16},{1,21},{... | collective-permute-start | bytes 24584 | tf_op jit(solution)/shard_map/ppermute | solution.py:18
  3.3 0.2 collective-permute-start.4
  3.5 1.1 %collective-permute-start.3 = (f32[8,16,16]{2,1,0:T(8,128)}, f32[8,16,16]{2,1,0:T(8,128)S(1)}, u32[]{:S(2)}, u32[]{:S(2)}) collective-permute-start(f32[8,16,16]{2,1,0:T(8,128)} %bitcast.23), channel_id=1, source_target_pairs={{0,28},{4,0},{8,4},{12,8},{16,12},{20,16},{24,20},{28,24},{1,29},{... | collective-permute-start | bytes 24584 | tf_op jit(solution)/shard_map/ppermute | solution.py:18
  4.6 1.3 %collective-permute-start.2 = (f32[8,16,16]{2,1,0:T(8,128)}, f32[8,16,16]{2,1,0:T(8,128)S(1)}, u32[]{:S(2)}, u32[]{:S(2)}) collective-permute-start(f32[8,16,16]{2,1,0:T(8,128)} %bitcast.24), channel_id=1, source_target_pairs={{0,4},{4,8},{8,12},{12,16},{16,20},{20,24},{24,28},{28,0},{1,5},{5... | collective-permute-start | bytes 24584 | tf_op jit(solution)/shard_map/ppermute | solution.py:18
  5.8 1.3 %collective-permute-start.1 = (f32[8,16,16]{2,1,0:T(8,128)}, f32[8,16,16]{2,1,0:T(8,128)S(1)}, u32[]{:S(2)}, u32[]{:S(2)}) collective-permute-start(f32[8,16,16]{2,1,0:T(8,128)} %bitcast.25), channel_id=1, source_target_pairs={{0,8},{4,12},{8,16},{12,20},{16,24},{20,28},{24,0},{28,4},{1,9},{5... | collective-permute-start | bytes 24584 | tf_op jit(solution)/shard_map/ppermute | solution.py:18
  7.1 0.0 collective-permute-done.5.refs_6_
  7.1 0.0 collective-permute-start
  7.2 0.7 %fusion.5.idx_ref = s32[8,64]{1,0:T(8,128)S(1)} fusion(s32[8,64]{1,0:T(8,128)} %param.10, s32[8,64]{1,0:T(8,128)} %param.11, s32[]{:T(128)S(6)} %axis_index.25), kind=kLoop, calls=%fused_computation.21 | loop fusion | flops 18432 | bytes 6148 | tf_op jit(solution)/shard_map/jit(_where)/select_n | solution.py:147
  7.9 0.9 %copy.8 = f32[8,16,16]{2,1,0:T(8,128)S(1)} copy(f32[8,16,16]{1,2,0:T(8,128)} %bitcast.27) | data formatting | bytes 16384
  8.8 0.0 collective-permute-done.4.refs_5_
  8.8 0.0 collective-permute-done.3.refs_4_
  8.8 0.0 collective-permute-done.2.refs_2_
  8.9 2.2 %collective-permute-done.1.refs_1_ = f32[8,16,16]{2,1,0:T(8,128)S(1)} collective-permute-done((f32[8,16,16]{2,1,0:T(8,128)}, f32[8,16,16]{2,1,0:T(8,128)S(1)}, u32[]{:S(2)}, u32[]{:S(2)}) %collective-permute-start.1) | collective-permute-done | bytes 8224 | tf_op jit(solution)/shard_map/ppermute | solution.py:18
  11.1 2.7 %collective-permute-done.refs_0_ = f32[8,16,16]{2,1,0:T(8,128)S(1)} collective-permute-done((f32[8,16,16]{2,1,0:T(8,128)}, f32[8,16,16]{2,1,0:T(8,128)S(1)}, u32[]{:S(2)}, u32[]{:S(2)}) %collective-permute-start) | collective-permute-done | bytes 8224 | tf_op jit(solution)/shard_map/ppermute | solution.py:18
  13.8 0.0 copy-start.1
  13.8 0.8 %copy-done.1 = f32[1,8,16,16]{3,2,1,0:T(8,128)S(1)} copy-done((f32[1,8,16,16]{3,2,1,0:T(8,128)S(1)}, f32[1,8,16,16]{3,2,1,0:T(8,128)}, u32[]{:S(2)}) %copy-start.1) | copy-done | bytes 8216
  14.7 25.8 %zone.1 = f32[7,16,128]{2,1,0:T(8,128)S(1)} custom-call(s32[8,64]{1,0:T(8,128)S(1)} %fusion.5.idx_ref, f32[8,16,256]{2,1,0:T(8,128)S(1)} %pad.4.clone.first_ref, bf16[8,1024,1024]{2,1,0:T(8,128)(2,1)} %bitcast.29, f32[8,16,16]{2,1,0:T(8,128)S(1)} %collective-permute-done.refs_0_, f32[8,16,16]{2,1,0:T(8,128)S(1)} %collective-permute-done.1.refs_1_, ...), custom_call_target="tpu_custom_call" | custom-call | tf_op jit(solution)/shard_map/zone/pallas_call | solution.py:153
  40.5 2.3 %collective-permute-start.11 = (f32[16,128]{1,0:T(8,128)S(1)}, f32[16,128]{1,0:T(8,128)S(1)}, u32[]{:S(2)}, u32[]{:S(2)}) collective-permute-start(f32[16,128]{1,0:T(8,128)S(1)} %get-tuple-element.13), channel_id=1, source_target_pairs={{0,12},{4,16},{8,20},{12,24},{16,28},{20,0},{24,4},{28,8},{1,13},{... | collective-permute-start | bytes 24584 | tf_op jit(solution)/shard_map/ppermute | solution.py:18
  42.8 0.5 collective-permute-start.10
  43.3 2.3 %collective-permute-start.9 = (f32[16,128]{1,0:T(8,128)S(1)}, f32[16,128]{1,0:T(8,128)S(1)}, u32[]{:S(2)}, u32[]{:S(2)}) collective-permute-start(f32[16,128]{1,0:T(8,128)S(1)} %get-tuple-element.15), channel_id=1, source_target_pairs={{0,4},{4,8},{8,12},{12,16},{16,20},{20,24},{24,28},{28,0},{1,5},{5... | collective-permute-start | bytes 24584 | tf_op jit(solution)/shard_map/ppermute | solution.py:18
  45.6 0.0 collective-permute-start.8
  45.6 1.9 %collective-permute-start.7 = (f32[16,128]{1,0:T(8,128)S(1)}, f32[16,128]{1,0:T(8,128)S(1)}, u32[]{:S(2)}, u32[]{:S(2)}) collective-permute-start(f32[16,128]{1,0:T(8,128)S(1)} %get-tuple-element.17), channel_id=1, source_target_pairs={{0,24},{4,28},{8,0},{12,4},{16,8},{20,12},{24,16},{28,20},{1,25},{... | collective-permute-start | bytes 24584 | tf_op jit(solution)/shard_map/ppermute | solution.py:18
  47.6 0.0 collective-permute-done.11.refs_6_
  47.6 1.3 %collective-permute-start.6 = (f32[16,128]{1,0:T(8,128)S(1)}, f32[16,128]{1,0:T(8,128)S(1)}, u32[]{:S(2)}, u32[]{:S(2)}) collective-permute-start(f32[16,128]{1,0:T(8,128)S(1)} %get-tuple-element.18), channel_id=1, source_target_pairs={{0,20},{4,24},{8,28},{12,0},{16,4},{20,8},{24,12},{28,16},{1,21},{... | collective-permute-start | bytes 24584 | tf_op jit(solution)/shard_map/ppermute | solution.py:18
  49.5 0.0 collective-permute-done.10.refs_5_
  49.6 0.0 collective-permute-done.9.refs_4_
  49.6 0.0 collective-permute-done.8.refs_3_
  49.6 0.0 collective-permute-done.7.refs_2_
  49.6 2.3 %collective-permute-done.6.refs_1_ = f32[16,128]{1,0:T(8,128)S(1)} collective-permute-done((f32[16,128]{1,0:T(8,128)S(1)}, f32[16,128]{1,0:T(8,128)S(1)}, u32[]{:S(2)}, u32[]{:S(2)}) %collective-permute-start.6) | collective-permute-done | bytes 8224 | tf_op jit(solution)/shard_map/ppermute | solution.py:18
  51.9 0.0 copy-done
  51.9 0.3 density.1
  52.1 4.7 %collective-permute-start.12 = (f32[8,256]{1,0:T(8,128)S(1)}, f32[8,256]{1,0:T(8,128)S(1)}, u32[]{:S(2)}, u32[]{:S(2)}) collective-permute-start(f32[8,256]{1,0:T(8,128)S(1)} %get-tuple-element.10), channel_id=1, source_target_pairs={{0,1},{1,2},{2,3},{3,0},{4,5},{5,6},{6,7},{7,4},{8,9},{9,10},{10,1... | collective-permute-start | bytes 24584 | tf_op jit(solution)/shard_map/ppermute | solution.py:18
  56.8 1.2 %collective-permute-start.13 = (f32[8,256]{1,0:T(8,128)S(1)}, f32[8,256]{1,0:T(8,128)S(1)}, u32[]{:S(2)}, u32[]{:S(2)}) collective-permute-start(f32[8,256]{1,0:T(8,128)S(1)} %get-tuple-element.11), channel_id=1, source_target_pairs={{0,2},{1,3},{2,0},{3,1},{4,6},{5,7},{6,4},{7,5},{8,10},{9,11},{10,... | collective-permute-start | bytes 24584 | tf_op jit(solution)/shard_map/ppermute | solution.py:18
  58.1 0.0 collective-permute-start.14
  58.1 0.0 collective-permute-done.12
  58.1 1.3 %collective-permute-done.13 = f32[8,256]{1,0:T(8,128)S(1)} collective-permute-done((f32[8,256]{1,0:T(8,128)S(1)}, f32[8,256]{1,0:T(8,128)S(1)}, u32[]{:S(2)}, u32[]{:S(2)}) %collective-permute-start.13) | collective-permute-done | bytes 8224 | tf_op jit(solution)/shard_map/ppermute | solution.py:18
  59.4 1.7 %collective-permute-done.14 = f32[8,256]{1,0:T(8,128)S(1)} collective-permute-done((f32[8,256]{1,0:T(8,128)S(1)}, f32[8,256]{1,0:T(8,128)S(1)}, u32[]{:S(2)}, u32[]{:S(2)}) %collective-permute-start.14) | collective-permute-done | bytes 8224 | tf_op jit(solution)/shard_map/ppermute | solution.py:18
  61.1 0.6 add_add_fusion
  (2 shorter events, 0.0 us)
Async XLA Ops:
  0.0 51.9 %copy-start = (bf16[1,8,16,1024]{3,2,1,0:T(8,128)(2,1)S(1)}, bf16[1,8,16,1024]{3,2,1,0:T(8,128)(2,1)}, u32[]{:S(2)}) copy-start(bf16[1,8,16,1024]{3,2,1,0:T(8,128)(2,1)} %param.8) | copy-start | bytes 786436
  0.0 7.1 %collective-permute-start.5 = (f32[8,16,16]{2,1,0:T(8,128)}, f32[8,16,16]{2,1,0:T(8,128)S(1)}, u32[]{:S(2)}, u32[]{:S(2)}) collective-permute-start(f32[8,16,16]{2,1,0:T(8,128)} %bitcast.21), channel_id=1, source_target_pairs={{0,20},{4,24},{8,28},{12,0},{16,4},{20,8},{24,12},{28,16},{1,21},{... | collective-permute-start | bytes 24584 | tf_op jit(solution)/shard_map/ppermute | solution.py:18
  3.3 5.5 %collective-permute-start.4 = (f32[8,16,16]{2,1,0:T(8,128)}, f32[8,16,16]{2,1,0:T(8,128)S(1)}, u32[]{:S(2)}, u32[]{:S(2)}) collective-permute-start(f32[8,16,16]{2,1,0:T(8,128)} %bitcast.22), channel_id=1, source_target_pairs={{0,24},{4,28},{8,0},{12,4},{16,8},{20,12},{24,16},{28,20},{1,25},{... | collective-permute-start | bytes 24584 | tf_op jit(solution)/shard_map/ppermute | solution.py:18
  3.5 5.4 %collective-permute-start.3 = (f32[8,16,16]{2,1,0:T(8,128)}, f32[8,16,16]{2,1,0:T(8,128)S(1)}, u32[]{:S(2)}, u32[]{:S(2)}) collective-permute-start(f32[8,16,16]{2,1,0:T(8,128)} %bitcast.23), channel_id=1, source_target_pairs={{0,28},{4,0},{8,4},{12,8},{16,12},{20,16},{24,20},{28,24},{1,29},{... | collective-permute-start | bytes 24584 | tf_op jit(solution)/shard_map/ppermute | solution.py:18
  4.6 4.3 %collective-permute-start.2 = (f32[8,16,16]{2,1,0:T(8,128)}, f32[8,16,16]{2,1,0:T(8,128)S(1)}, u32[]{:S(2)}, u32[]{:S(2)}) collective-permute-start(f32[8,16,16]{2,1,0:T(8,128)} %bitcast.24), channel_id=1, source_target_pairs={{0,4},{4,8},{8,12},{12,16},{16,20},{20,24},{24,28},{28,0},{1,5},{5... | collective-permute-start | bytes 24584 | tf_op jit(solution)/shard_map/ppermute | solution.py:18
  5.8 5.2 %collective-permute-start.1 = (f32[8,16,16]{2,1,0:T(8,128)}, f32[8,16,16]{2,1,0:T(8,128)S(1)}, u32[]{:S(2)}, u32[]{:S(2)}) collective-permute-start(f32[8,16,16]{2,1,0:T(8,128)} %bitcast.25), channel_id=1, source_target_pairs={{0,8},{4,12},{8,16},{12,20},{16,24},{20,28},{24,0},{28,4},{1,9},{5... | collective-permute-start | bytes 24584 | tf_op jit(solution)/shard_map/ppermute | solution.py:18
  7.1 6.7 %collective-permute-start = (f32[8,16,16]{2,1,0:T(8,128)}, f32[8,16,16]{2,1,0:T(8,128)S(1)}, u32[]{:S(2)}, u32[]{:S(2)}) collective-permute-start(f32[8,16,16]{2,1,0:T(8,128)} %bitcast.26), channel_id=1, source_target_pairs={{0,12},{4,16},{8,20},{12,24},{16,28},{20,0},{24,4},{28,8},{1,13},{... | collective-permute-start | bytes 24584 | tf_op jit(solution)/shard_map/ppermute | solution.py:18
  13.8 0.8 %copy-start.1 = (f32[1,8,16,16]{3,2,1,0:T(8,128)S(1)}, f32[1,8,16,16]{3,2,1,0:T(8,128)}, u32[]{:S(2)}) copy-start(f32[1,8,16,16]{3,2,1,0:T(8,128)} %param.6) | copy-start | bytes 24580
  40.5 7.0 %collective-permute-start.11 = (f32[16,128]{1,0:T(8,128)S(1)}, f32[16,128]{1,0:T(8,128)S(1)}, u32[]{:S(2)}, u32[]{:S(2)}) collective-permute-start(f32[16,128]{1,0:T(8,128)S(1)} %get-tuple-element.13), channel_id=1, source_target_pairs={{0,12},{4,16},{8,20},{12,24},{16,28},{20,0},{24,4},{28,8},{1,13},{... | collective-permute-start | bytes 24584 | tf_op jit(solution)/shard_map/ppermute | solution.py:18
  42.8 6.7 %collective-permute-start.10 = (f32[16,128]{1,0:T(8,128)S(1)}, f32[16,128]{1,0:T(8,128)S(1)}, u32[]{:S(2)}, u32[]{:S(2)}) collective-permute-start(f32[16,128]{1,0:T(8,128)S(1)} %get-tuple-element.14), channel_id=1, source_target_pairs={{0,8},{4,12},{8,16},{12,20},{16,24},{20,28},{24,0},{28,4},{1,9},{5... | collective-permute-start | bytes 24584 | tf_op jit(solution)/shard_map/ppermute | solution.py:18
  43.3 6.2 %collective-permute-start.9 = (f32[16,128]{1,0:T(8,128)S(1)}, f32[16,128]{1,0:T(8,128)S(1)}, u32[]{:S(2)}, u32[]{:S(2)}) collective-permute-start(f32[16,128]{1,0:T(8,128)S(1)} %get-tuple-element.15), channel_id=1, source_target_pairs={{0,4},{4,8},{8,12},{12,16},{16,20},{20,24},{24,28},{28,0},{1,5},{5... | collective-permute-start | bytes 24584 | tf_op jit(solution)/shard_map/ppermute | solution.py:18
  45.6 3.9 %collective-permute-start.8 = (f32[16,128]{1,0:T(8,128)S(1)}, f32[16,128]{1,0:T(8,128)S(1)}, u32[]{:S(2)}, u32[]{:S(2)}) collective-permute-start(f32[16,128]{1,0:T(8,128)S(1)} %get-tuple-element.16), channel_id=1, source_target_pairs={{0,28},{4,0},{8,4},{12,8},{16,12},{20,16},{24,20},{28,24},{1,29},{... | collective-permute-start | bytes 24584 | tf_op jit(solution)/shard_map/ppermute | solution.py:18
  45.6 4.0 %collective-permute-start.7 = (f32[16,128]{1,0:T(8,128)S(1)}, f32[16,128]{1,0:T(8,128)S(1)}, u32[]{:S(2)}, u32[]{:S(2)}) collective-permute-start(f32[16,128]{1,0:T(8,128)S(1)} %get-tuple-element.17), channel_id=1, source_target_pairs={{0,24},{4,28},{8,0},{12,4},{16,8},{20,12},{24,16},{28,20},{1,25},{... | collective-permute-start | bytes 24584 | tf_op jit(solution)/shard_map/ppermute | solution.py:18
  47.6 4.3 %collective-permute-start.6 = (f32[16,128]{1,0:T(8,128)S(1)}, f32[16,128]{1,0:T(8,128)S(1)}, u32[]{:S(2)}, u32[]{:S(2)}) collective-permute-start(f32[16,128]{1,0:T(8,128)S(1)} %get-tuple-element.18), channel_id=1, source_target_pairs={{0,20},{4,24},{8,28},{12,0},{16,4},{20,8},{24,12},{28,16},{1,21},{... | collective-permute-start | bytes 24584 | tf_op jit(solution)/shard_map/ppermute | solution.py:18
  52.1 5.9 %collective-permute-start.12 = (f32[8,256]{1,0:T(8,128)S(1)}, f32[8,256]{1,0:T(8,128)S(1)}, u32[]{:S(2)}, u32[]{:S(2)}) collective-permute-start(f32[8,256]{1,0:T(8,128)S(1)} %get-tuple-element.10), channel_id=1, source_target_pairs={{0,1},{1,2},{2,3},{3,0},{4,5},{5,6},{6,7},{7,4},{8,9},{9,10},{10,1... | collective-permute-start | bytes 24584 | tf_op jit(solution)/shard_map/ppermute | solution.py:18
  56.8 2.6 %collective-permute-start.13 = (f32[8,256]{1,0:T(8,128)S(1)}, f32[8,256]{1,0:T(8,128)S(1)}, u32[]{:S(2)}, u32[]{:S(2)}) collective-permute-start(f32[8,256]{1,0:T(8,128)S(1)} %get-tuple-element.11), channel_id=1, source_target_pairs={{0,2},{1,3},{2,0},{3,1},{4,6},{5,7},{6,4},{7,5},{8,10},{9,11},{10,... | collective-permute-start | bytes 24584 | tf_op jit(solution)/shard_map/ppermute | solution.py:18
  58.1 3.1 %collective-permute-start.14 = (f32[8,256]{1,0:T(8,128)S(1)}, f32[8,256]{1,0:T(8,128)S(1)}, u32[]{:S(2)}, u32[]{:S(2)}) collective-permute-start(f32[8,256]{1,0:T(8,128)S(1)} %get-tuple-element.12), channel_id=1, source_target_pairs={{0,3},{1,0},{2,1},{3,2},{4,7},{5,4},{6,5},{7,6},{8,11},{9,8},{10,9... | collective-permute-start | bytes 24584 | tf_op jit(solution)/shard_map/ppermute | solution.py:18
